TPU v7x, 32 devices: a whole 2x2x4 slice. The times are simulated.
32 devices in a mesh: row: 16 (over z, x, core), col: 2 (over y).
Axes of the slice: x: 2, y: 2, z: 4, core: 2. Of those that a mesh axis runs over, the one named last changes fastest.
Arguments:
- tokens: bfloat16 [1024, 8192], P('row', 'col'), may hold values from -6 to 6
- norm_gain: bfloat16 [8192], P('col'), may hold values from 0.099609375 to 1.8984375
- gate_proj: bfloat16 [8192, 28672], P('col', 'row'), may hold values from -0.0625 to 0.0625
- up_proj: bfloat16 [8192, 28672], P('col', 'row'), may hold values from -0.0625 to 0.0625
- down_proj: bfloat16 [28672, 8192], P('row', 'col'), may hold values from -0.03125 to 0.03125
Outputs:
- mixed: bfloat16 [1024, 8192], P('row', 'col')
All inputs are finite; a program needn't handle non-finite values.
Results may differ from a plain program's by a relative error of at most 0.015.
Values may be sent and summed in bfloat16 or wider, within the bound.
A program may use at most 128 MiB of HBM per device.

v0:
```python
import jax
import jax.numpy as jnp
from jax import lax
from jax.sharding import PartitionSpec as P

D = 8192


floor_term = 0.25


def shards(tokens, norm_gain, gate_proj, up_proj, down_proj):
    gathered = lax.all_gather(tokens, "row", axis=0, tiled=True)
    widened = gathered.astype(jnp.float32)
    partial_squares = jnp.sum(widened * widened, axis=1)
    scaled = (widened * norm_gain.astype(jnp.float32)[None, :]).astype(jnp.bfloat16)
    gate_part = jnp.dot(scaled, gate_proj, preferred_element_type=jnp.float32)
    up_part = jnp.dot(scaled, up_proj, preferred_element_type=jnp.float32)
    gate_sum, up_sum, block_squares = (
        lax.psum_scatter(
            gate_part.astype(jnp.bfloat16), "col", scatter_dimension=0, tiled=True
        ).astype(jnp.float32),
        lax.psum_scatter(
            up_part.astype(jnp.bfloat16), "col", scatter_dimension=0, tiled=True
        ).astype(jnp.float32),
        lax.psum_scatter(
            partial_squares.astype(jnp.bfloat16), "col", scatter_dimension=0, tiled=True
        ).astype(jnp.float32),
    )
    row_scale = 1.0 / jnp.sqrt(block_squares / D + floor_term)
    gate_value = row_scale[:, None] * gate_sum
    up_value = row_scale[:, None] * up_sum
    hidden = (jax.nn.silu(gate_value) * up_value).astype(jnp.bfloat16)
    partial_out = jnp.dot(
        lax.all_gather(hidden, "col", axis=0, tiled=True),
        down_proj,
        preferred_element_type=jnp.float32,
    )
    summed = lax.psum_scatter(
        partial_out.astype(jnp.bfloat16), "row", scatter_dimension=0, tiled=True
    ).astype(jnp.float32)
    return (tokens.astype(jnp.float32) + summed).astype(jnp.bfloat16)


def solution(mesh):
    in_specs = (P("row", "col"), P("col"), P("col", "row"), P("col", "row"), P("row", "col"))
    out_specs = P("row", "col")
    return jax.shard_map(shards, mesh=mesh, in_specs=in_specs, out_specs=out_specs, check_vma=False)
```

profile of v0, /device:TPU:0, one launch (start us, length us, event | category | flops | bytes accessed | tf_op | source)
XLA Modules:
  0.0 398.2 jit_solution(12197381151553186310)
XLA Ops:
  6.5 0.0 all-gather.3.cloned.1.call-start
  6.5 0.7 all-gather.3.cloned.1.call-update
  7.3 0.0 reduce-scatter.4.cloned.1.call-start
  7.3 0.7 convert_element_type.46
  8.0 78.5 %all-gather.3.cloned.1.call-done = bf16[1024,4096]{1,0:T(8,128)(2,1)} async-done(((bf16[64,4096]{1,0:T(8,128)(2,1)}), bf16[1024,4096]{1,0:T(8,128)(2,1)}) %all-gather.3.cloned.1.call-update) | async-done | bytes 8388624 | tf_op jit(solution)/shard_map/all_gather | solution.py:13
  86.5 22.6 %fusion.6 = bf16[1024,1792]{1,0:T(8,128)(2,1)} fusion(bf16[4096,1792]{1,0:T(8,128)(2,1)} %param.7, bf16[1024,4096]{1,0:T(8,128)(2,1)} %all-gather.3.cloned.1.call-done, f32[4096]{0:T(1024)S(1)} %convert_element_type.46), kind=kOutput, calls=%fused_computation.7 | convolution fusion | flops 15046803456 | bytes 26755072 | tf_op jit(solution)/shard_map/dot_general | solution.py:17
  109.1 0.0 reduce-scatter.4.cloned.1.call-update
  109.2 0.0 copy-start.1
  109.2 0.0 reduce-scatter.6.cloned.1.call-start
  109.2 23.8 %fusion.9 = bf16[1024,1792]{1,0:T(8,128)(2,1)} fusion(bf16[4096,1792]{1,0:T(8,128)(2,1)} %param.8, bf16[1024,4096]{1,0:T(8,128)(2,1)} %all-gather.3.cloned.1.call-done, f32[4096]{0:T(1024)S(1)} %convert_element_type.46), kind=kOutput, calls=%fused_computation.8 | convolution fusion | flops 15046803456 | bytes 26755072 | tf_op jit(solution)/shard_map/dot_general | solution.py:18
  133.0 0.0 reduce-scatter.6.cloned.1.call-update
  133.0 0.0 all-gather.5.cloned.1.call-start
  133.1 0.0 copy-done.1
  133.1 0.6 dynamic-slice
  134.3 5.1 %fusion = bf16[1024]{0:T(1024)(128)(2,1)S(1)} fusion(bf16[1024,4096]{1,0:T(8,128)(2,1)} %all-gather.3.cloned.1.call-done), kind=kLoop, calls=%fused_computation.2 | loop fusion | flops 12581888 | bytes 8390656 | tf_op jit(solution)/shard_map/reduce_sum | solution.py:15
  139.4 5.1 %all-reduce = bf16[1024]{0:T(1024)(128)(2,1)S(1)} all-reduce(bf16[1024]{0:T(1024)(128)(2,1)S(1)} %fusion), channel_id=2, replica_groups=mesh['row'=16,'col'=2] {'col'}, use_global_device_ids=true, to_apply=%region_1.0.clone | all-reduce | flops 1024 | bytes 4096
  144.6 0.1 add_rsqrt_fusion
  144.6 12.5 %reduce-scatter.4.cloned.1.call-done = bf16[512,1792]{1,0:T(8,128)(2,1)} async-done(((bf16[1024,1792]{1,0:T(8,128)(2,1)}), bf16[512,1792]{1,0:T(8,128)(2,1)}) %reduce-scatter.4.cloned.1.call-update) | async-done | bytes 1835024 | tf_op jit(solution)/shard_map/reduce_scatter | solution.py:20
  157.2 51.5 %reduce-scatter.6.cloned.1.call-done = bf16[512,1792]{1,0:T(8,128)(2,1)} async-done(((bf16[1024,1792]{1,0:T(8,128)(2,1)}), bf16[512,1792]{1,0:T(8,128)(2,1)}) %reduce-scatter.6.cloned.1.call-update) | async-done | bytes 1835024 | tf_op jit(solution)/shard_map/reduce_scatter | solution.py:23
  208.6 4.7 %multiply_convert_fusion = bf16[512,1792]{1,0:T(8,128)(2,1)} fusion(bf16[512,1792]{1,0:T(8,128)(2,1)} %reduce-scatter.6.cloned.1.call-done, bf16[512,1792]{1,0:T(8,128)(2,1)} %reduce-scatter.4.cloned.1.call-done, f32[512]{0:T(512)S(1)} %add_rsqrt_fusion), kind=kLoop, calls=%fused_computation.9 | loop fusion | flops 9175040 | bytes 5507072 | tf_op jit(solution)/shard_map/convert_element_type | solution.py:33
  213.4 0.0 all-gather.5.cloned.1.call-update
  213.4 0.2 reduce-scatter.8.cloned.1.call-start
  213.6 50.7 %all-gather.5.cloned.1.call-done = bf16[1024,1792]{1,0:T(8,128)(2,1)} async-done(((bf16[512,1792]{1,0:T(8,128)(2,1)}), bf16[1024,1792]{1,0:T(8,128)(2,1)}) %all-gather.5.cloned.1.call-update) | async-done | bytes 3670032 | tf_op jit(solution)/shard_map/all_gather | solution.py:35
  264.3 21.7 %convolution_convert_fusion = bf16[1024,4096]{1,0:T(8,128)(2,1)} fusion(bf16[1024,1792]{1,0:T(8,128)(2,1)} %all-gather.5.cloned.1.call-done, bf16[1792,4096]{1,0:T(8,128)(2,1)} %param.9), kind=kOutput, calls=%fused_computation.4 | convolution fusion | flops 15036579840 | bytes 26738688 | tf_op jit(solution)/shard_map/dot_general | solution.py:34
  286.1 0.0 copy-start
  286.1 0.0 reduce-scatter.8.cloned.1.call-update
  286.1 103.6 %reduce-scatter.8.cloned.1.call-done = bf16[64,4096]{1,0:T(8,128)(2,1)} async-done(((bf16[1024,4096]{1,0:T(8,128)(2,1)}), bf16[64,4096]{1,0:T(8,128)(2,1)}) %reduce-scatter.8.cloned.1.call-update) | async-done | bytes 524304 | tf_op jit(solution)/shard_map/reduce_scatter | solution.py:39
  389.7 0.0 copy-done
  389.7 2.0 add_convert_fusion
Async XLA Ops:
  6.5 80.0 %all-gather.3.cloned.1.call-start = ((), (), s32[]{:S(2)}) async-start(), calls=%async_computation.3 | async-start | bytes 8912896 | tf_op jit(solution)/shard_map/all_gather | solution.py:13
  7.3 149.9 %reduce-scatter.4.cloned.1.call-start = ((), (), s32[]{:S(2)}) async-start(), calls=%async_computation.4 | async-start | bytes 5505024 | tf_op jit(solution)/shard_map/reduce_scatter | solution.py:20
  109.2 23.9 %copy-start.1 = (u32[32]{0:T(128)S(1)}, u32[32]{0:T(128)}, u32[]{:S(2)}) copy-start(u32[32]{0:T(128)} %constant.13) | copy-start | bytes 388
  109.2 99.5 %reduce-scatter.6.cloned.1.call-start = ((), (), s32[]{:S(2)}) async-start(), calls=%async_computation.5 | async-start | bytes 5505024 | tf_op jit(solution)/shard_map/reduce_scatter | solution.py:23
  133.0 131.3 %all-gather.5.cloned.1.call-start = ((), (), s32[]{:S(2)}) async-start(), calls=%async_computation.6 | async-start | bytes 5505024 | tf_op jit(solution)/shard_map/all_gather | solution.py:35
  213.4 176.3 %reduce-scatter.8.cloned.1.call-start = ((), (), s32[]{:S(2)}) async-start(), calls=%async_computation.7 | async-start | bytes 8912896 | tf_op jit(solution)/shard_map/reduce_scatter | solution.py:39
  286.1 103.6 %copy-start = (bf16[64,4096]{1,0:T(8,128)(2,1)S(1)}, bf16[64,4096]{1,0:T(8,128)(2,1)}, u32[]{:S(2)}) copy-start(bf16[64,4096]{1,0:T(8,128)(2,1)} %param.5) | copy-start | bytes 1572868
Sparse Core Ops, SparseCore 0:
  9.5 77.0 all-gather.2
  109.3 47.8 reduce-scatter.3
  159.4 49.1 reduce-scatter.5
  213.5 50.7 all-gather.4
  286.2 103.4 reduce-scatter.7
where the time goes:
time: 398 us
  waiting for transfers between devices  298 us (75%)
  matrix products  68.1 us (17%)
  between operations  13.8 us (3%)
  other arithmetic  12.6 us (3%)
  blocking collectives  5.14 us (1%)
    reduce_scatter x1, waiting for transfers between devices, shards(): lax.psum_scatter(partial_out.astype(jnp.bfloat16), 'row', scatter_dimensi...  104 us
    all_gather x1, waiting for transfers between devices, shards(): gathered = lax.all_gather(tokens, 'row', axis=0, tiled=True)  78.5 us
    reduce_scatter x1, waiting for transfers between devices, shards(): lax.psum_scatter(up_part.astype(jnp.bfloat16), 'col', scatter_dimension=0...  51.5 us
    all_gather x1, waiting for transfers between devices, shards(): lax.all_gather(hidden, 'col', axis=0, tiled=True)  50.7 us
    dot_general x1, matrix products, shards(): up_part = jnp.dot(scaled, up_proj, preferred_element_type=jnp.float32)  23.8 us
    dot_general x1, matrix products, shards(): gate_part = jnp.dot(scaled, gate_proj, preferred_element_type=jnp.float32)  22.6 us
    dot_general x1, matrix products, shards(): jnp.dot(lax.all_gather(hidden, 'col', axis=0, tiled=True), down_proj, pre...  21.7 us
    reduce_scatter x1, waiting for transfers between devices, shards(): lax.psum_scatter(gate_part.astype(jnp.bfloat16), 'col', scatter_dimension...  12.5 us
  transfers between devices with their start and end apart: 5, of which 5 were waited for; matrix products, arithmetic and copies ran while one was open for 8% of the time, Pallas kernels for 0%

commit v1 on v0

--- a/solution.py
+++ b/solution.py
@@ -1,15 +1,281 @@
+import functools
+
 import jax
 import jax.numpy as jnp
 from jax import lax
+from jax.experimental import pallas as pl
+from jax.experimental.pallas import tpu as pltpu
 from jax.sharding import PartitionSpec as P
 
-D = 8192
-
-
 floor_term = 0.25
-
-
-def shards(tokens, norm_gain, gate_proj, up_proj, down_proj):
+MESH = pl.DeviceIdType.MESH
+BF = jnp.bfloat16
+F32 = jnp.float32
+
+
+def places(rows):
+    n = rows // 2
+    row, col = lax.axis_index("row"), lax.axis_index("col")
+    core, chip = row % 2, row // 2
+    z, x = chip // 2, chip % 2
+    pos = z + x * (n - 1 - 2 * z)
+
+    def at(p):
+        p = (p + n) % n
+        far = (2 * p) // n
+        return ((1 - far) * 2 * p + far * (2 * (n - 1 - p) + 1)) * 2 + core
+
+    right, left = (at(pos + 1), col), (at(pos - 1), col)
+    return core, col, right, left, (row + 1 - 2 * core, col), (row, 1 - col)
+
+
+def greet(partners):
+    barrier = pltpu.get_barrier_semaphore()
+    for device in partners:
+        pl.semaphore_signal(barrier, inc=1, device_id=device, device_id_type=MESH)
+    pl.semaphore_wait(barrier, len(partners))
+
+
+def remote(src, dst, send, recv, device):
+    return pltpu.make_async_remote_copy(
+        src_ref=src, dst_ref=dst, send_sem=send, recv_sem=recv, device_id=device, device_id_type=MESH
+    )
+
+
+def first_kernel(rows, cols, tile, tok, gain, wg_hbm, wu_hbm, hid, wg, wu, x, pb, rv, sq, sq_in,
+                 w_sem, sq_sem, ring_s, ring_r, sib_s, sib_r, y_s, y_r):
+    n = rows // 2
+    half, width = tok.shape[0] // 2, tok.shape[1]
+    units = wg.shape[1]
+    load_g = pltpu.make_async_copy(wg_hbm, wg, w_sem.at[0])
+    load_u = pltpu.make_async_copy(wu_hbm, wu, w_sem.at[1])
+    load_g.start()
+    load_u.start()
+    core, col, right, left, sibling, across = places(rows)
+    wide = tok[...].astype(F32)
+    sq[...] = jnp.broadcast_to(jnp.sum(wide * wide, axis=1, keepdims=True), sq.shape)
+    greet((right, left, sibling, across))
+    sums = remote(sq, sq_in, sq_sem.at[0], sq_sem.at[1], across)
+    sums.start()
+    sums.wait()
+    total = sq[:, 0:1] + sq_in[:, 0:1]
+    scale = 1.0 / jnp.sqrt(total / (width * cols) + floor_term)
+    normed = (tok[...].astype(F32) * gain[...].astype(F32) * scale).astype(BF)
+    x[0, 0, core] = normed[:half]
+    x[0, 1, core] = normed[half:]
+
+    def ring(s, d):
+        return remote(x.at[s, d, core], x.at[s + 1, d, core], ring_s.at[s, d], ring_r.at[s, d], (right, left)[d])
+
+    def sib(s, d):
+        return remote(x.at[s, d, core], x.at[s, d, core], sib_s.at[s, d], sib_r.at[s, d], sibling)
+
+    def swap(s, g):
+        return remote(pb.at[s, g, 1 - col], rv.at[s, g], y_s.at[s, g], y_r.at[s, g], across)
+
+    def product(s, g, w):
+        @pl.loop(0, units // tile)
+        def _(t):
+            at = pl.ds(pl.multiple_of(t * tile, tile), tile)
+            part = jnp.dot(x[s].reshape(4 * half, width), w[:, at], preferred_element_type=F32)
+            pb[s, g, :, :, at] = part.astype(BF).reshape(2, 2 * half, tile)
+        swap(s, g).start()
+
+    def finish(s):
+        swap(s, 0).wait_recv()
+        swap(s, 1).wait_recv()
+
+        @pl.loop(0, units // tile)
+        def _(t):
+            at = pl.ds(pl.multiple_of(t * tile, tile), tile)
+            gate = pb[s, 0, col, :, at].astype(F32) + rv[s, 0, :, at].astype(F32)
+            up = pb[s, 1, col, :, at].astype(F32) + rv[s, 1, :, at].astype(F32)
+            hid[s, :, at] = (gate / (1.0 + jnp.exp(-gate)) * up).astype(BF)
+
+    @pl.loop(0, n)
+    def _(s):
+        @pl.when(s > 0)
+        def _():
+            ring(s - 1, 0).wait_recv()
+            ring(s - 1, 1).wait_recv()
+
+        @pl.when(s < n - 1)
+        def _():
+            ring(s, 0).start()
+            ring(s, 1).start()
+
+        sib(s, 0).start()
+        sib(s, 1).start()
+        sib(s, 0).wait_recv()
+        sib(s, 1).wait_recv()
+
+        @pl.when(s == 0)
+        def _():
+            load_g.wait()
+
+        product(s, 0, wg)
+
+        @pl.when(s == 0)
+        def _():
+            load_u.wait()
+
+        product(s, 1, wu)
+
+        @pl.when(s > 1)
+        def _():
+            finish(s - 2)
+
+    @pl.loop(n - 2, n)
+    def _(s):
+        finish(s)
+
+    @pl.loop(0, n)
+    def _(s):
+        for d in range(2):
+            sib(s, d).wait_send()
+            swap(s, d).wait_send()
+
+        @pl.when(s < n - 1)
+        def _():
+            ring(s, 0).wait_send()
+            ring(s, 1).wait_send()
+
+
+def second_kernel(rows, tile, hid, tok, wd_hbm, out, wd, hb, pb, r1, rr, sn,
+                  w_sem, h_sem, y_s, y_r, sib_s, sib_r, ring_s, ring_r):
+    n = rows // 2
+    half, width = tok.shape[0] // 2, tok.shape[1]
+    piece = width // 2
+    units = wd.shape[0]
+    core, col, right, left, sibling, across = places(rows)
+    load = pltpu.make_async_copy(wd_hbm, wd, w_sem)
+    load.start()
+    mine = pltpu.make_async_copy(hid, hb.at[col], h_sem)
+    mine.start()
+    rr[n - 1] = jnp.zeros(rr.shape[1:], BF)
+    greet((right, left, sibling, across))
+    mine.wait()
+
+    def swap(s):
+        return remote(hb.at[col, s], hb.at[col, s], y_s.at[s], y_r.at[s], across)
+
+    def sib(s, d):
+        return remote(pb.at[s, d, 1 - core], r1.at[s, d], sib_s.at[s, d], sib_r.at[s, d], sibling)
+
+    def ring(s, d, k):
+        return remote(sn.at[s, d, k], rr.at[s - 1, d, k], ring_s.at[s, d, k], ring_r.at[s, d, k], (left, right)[d])
+
+    @pl.loop(0, n)
+    def _(i):
+        swap(n - 1 - i).start()
+
+    load.wait()
+
+    def product(s):
+        swap(s).wait_recv()
+
+        for k in range(2):
+            @pl.loop(0, piece // tile)
+            def _(t):
+                start = pl.multiple_of(t * tile, tile)
+                w = wd[:, pl.ds(pl.multiple_of(k * piece + t * tile, tile), tile)]
+                h = jnp.concatenate([hb[0, s], hb[1, s]], axis=0)
+                part = jnp.dot(h, w, preferred_element_type=F32).astype(BF)
+                pb[s, :, :, k, :, pl.ds(start, tile)] = part.reshape(2, 2, half, tile)
+        sib(s, 0).start()
+        sib(s, 1).start()
+
+    def added(s, d, k):
+        return pb[s, d, core, k].astype(F32) + r1[s, d, k].astype(F32) + rr[s, d, k].astype(F32)
+
+    product(n - 1)
+
+    @pl.loop(0, n - 1)
+    def _(i):
+        s = n - 1 - i
+        product(s - 1)
+        sib(s, 0).wait_recv()
+        sib(s, 1).wait_recv()
+        for k in range(2):
+            for d in range(2):
+                @pl.when(s < n - 1)
+                def _():
+                    ring(s + 1, d, k).wait_recv()
+
+                sn[s, d, k] = added(s, d, k).astype(BF)
+                ring(s, d, k).start()
+
+    sib(0, 0).wait_recv()
+    sib(0, 1).wait_recv()
+    for k in range(2):
+        for d in range(2):
+            ring(1, d, k).wait_recv()
+            here = (slice(d * half, (d + 1) * half), slice(k * piece, (k + 1) * piece))
+            out[here] = (tok[here].astype(F32) + added(0, d, k)).astype(BF)
+
+    @pl.loop(0, n)
+    def _(s):
+        swap(s).wait_send()
+        for d in range(2):
+            sib(s, d).wait_send()
+
+        @pl.when(s > 0)
+        def _():
+            for d in range(2):
+                for k in range(2):
+                    ring(s, d, k).wait_send()
+
+
+def kernels(rows, cols, tokens, norm_gain, gate_proj, up_proj, down_proj):
+    n = rows // 2
+    count, width = tokens.shape
+    half = count // 2
+    units = gate_proj.shape[1]
+    tile = 256 if units % 256 == 0 else 128
+    vmem, hbm = pl.BlockSpec(memory_space=pltpu.VMEM), pl.BlockSpec(memory_space=pl.ANY)
+    dma = pltpu.SemaphoreType.DMA
+    hidden = pl.pallas_call(
+        functools.partial(first_kernel, rows, cols, tile),
+        out_shape=jax.ShapeDtypeStruct((n, 2 * half, units), BF),
+        in_specs=[vmem, vmem, hbm, hbm],
+        out_specs=vmem,
+        scratch_shapes=[
+            pltpu.VMEM(gate_proj.shape, BF),
+            pltpu.VMEM(up_proj.shape, BF),
+            pltpu.VMEM((n, 2, 2, half, width), BF),
+            pltpu.VMEM((n, 2, 2, 2 * half, units), BF),
+            pltpu.VMEM((n, 2, 2 * half, units), BF),
+            pltpu.VMEM((count, 128), F32),
+            pltpu.VMEM((count, 128), F32),
+            dma((2,)), dma((2,)),
+            dma((n, 2)), dma((n, 2)), dma((n, 2)), dma((n, 2)), dma((n, 2)), dma((n, 2)),
+        ],
+        compiler_params=pltpu.CompilerParams(
+            collective_id=0, has_side_effects=True, vmem_limit_bytes=60 * 1024 * 1024
+        ),
+    )(tokens, norm_gain.reshape(1, width), gate_proj, up_proj)
+    return pl.pallas_call(
+        functools.partial(second_kernel, rows, 256),
+        out_shape=jax.ShapeDtypeStruct(tokens.shape, BF),
+        in_specs=[hbm, vmem, hbm],
+        out_specs=vmem,
+        scratch_shapes=[
+            pltpu.VMEM(down_proj.shape, BF),
+            pltpu.VMEM((2, n, 2 * half, units), BF),
+            pltpu.VMEM((n, 2, 2, 2, half, width // 2), BF),
+            pltpu.VMEM((n, 2, 2, half, width // 2), BF),
+            pltpu.VMEM((n, 2, 2, half, width // 2), BF),
+            pltpu.VMEM((n, 2, 2, half, width // 2), BF),
+            dma, dma,
+            dma((n,)), dma((n,)), dma((n, 2)), dma((n, 2)), dma((n, 2, 2)), dma((n, 2, 2)),
+        ],
+        compiler_params=pltpu.CompilerParams(
+            collective_id=1, has_side_effects=True, vmem_limit_bytes=60 * 1024 * 1024
+        ),
+    )(hidden, tokens, down_proj)
+
+
+def plain(rows, cols, tokens, norm_gain, gate_proj, up_proj, down_proj):
     gathered = lax.all_gather(tokens, "row", axis=0, tiled=True)
     widened = gathered.astype(jnp.float32)
     partial_squares = jnp.sum(widened * widened, axis=1)
@@ -27,7 +293,7 @@
             partial_squares.astype(jnp.bfloat16), "col", scatter_dimension=0, tiled=True
         ).astype(jnp.float32),
     )
-    row_scale = 1.0 / jnp.sqrt(block_squares / D + floor_term)
+    row_scale = 1.0 / jnp.sqrt(block_squares / (tokens.shape[1] * cols) + floor_term)
     gate_value = row_scale[:, None] * gate_sum
     up_value = row_scale[:, None] * up_sum
     hidden = (jax.nn.silu(gate_value) * up_value).astype(jnp.bfloat16)
@@ -43,6 +309,10 @@
 
 
 def solution(mesh):
+    rows, cols = mesh.shape["row"], mesh.shape["col"]
+    body = kernels if cols == 2 and rows % 4 == 0 and rows >= 8 else plain
     in_specs = (P("row", "col"), P("col"), P("col", "row"), P("col", "row"), P("row", "col"))
     out_specs = P("row", "col")
-    return jax.shard_map(shards, mesh=mesh, in_specs=in_specs, out_specs=out_specs, check_vma=False)
+    return jax.shard_map(
+        functools.partial(body, rows, cols), mesh=mesh, in_specs=in_specs, out_specs=out_specs, check_vma=False
+    )

time: 398 us -> 166 us (0.42)
  waiting for transfers between devices: 298 us -> 0 us
  Pallas kernels: 0 us -> 163 us
  matrix products: 68.1 us -> 0 us
  between operations: 13.8 us -> 0.02 us
  other arithmetic: 12.6 us -> 0 us
  blocking collectives: 5.14 us -> 0 us
    reduce_scatter x3 -> x0, waiting for transfers between devices: 168 us -> none  [the longest x1 104 us: shards(): lax.psum_scatter(partial_out.astype(jnp.bfloat16), 'row', scatter_dimensi...]
    pallas_call x0 -> x2, Pallas kernels: none -> 163 us  [the longest x1 94.9 us: kernels(): pl.pallas_call(functools.partial(first_kernel, rows, cols, tile), out_sha...]
    all_gather x2 -> x0, waiting for transfers between devices: 129 us -> none  [the longest x1 78.5 us: shards(): gathered = lax.all_gather(tokens, 'row', axis=0, tiled=True)]
    dot_general x3 -> x0, matrix products: 68.1 us -> none  [the longest x1 23.8 us: shards(): up_part = jnp.dot(scaled, up_proj, preferred_element_type=jnp.float32)]
    convert_element_type x3 -> x0, other arithmetic: 7.38 us -> none  [the longest x1 4.73 us: shards(): hidden = (jax.nn.silu(gate_value) * up_value).astype(jnp.bfloat16)]
    unnamed x1 -> x0, blocking collectives: 5.14 us -> none
    reduce_sum x1 -> x0, other arithmetic: 5.11 us -> none  [shards(): partial_squares = jnp.sum(widened * widened, axis=1)]
  transfers between devices with their start and end apart: 5 -> 0, of which waited for: 5 -> 0; matrix products, arithmetic and copies ran while one was open for 8% -> 0% of each run, Pallas kernels for 0% -> 0%
where the time goes in v1:
time: 166 us
  Pallas kernels  163 us (98%)
  local copies, waits for them, and re-layouts  3.18 us (2%)
    pallas_call x1, Pallas kernels, kernels(): pl.pallas_call(functools.partial(first_kernel, rows, cols, tile), out_sha...  94.9 us
    pallas_call x1, Pallas kernels, kernels(): pl.pallas_call(functools.partial(second_kernel, rows, 256), out_shape=jax...  68 us

profile of v1, /device:TPU:0, one launch (start us, length us, event | category | flops | bytes accessed | tf_op | source)
XLA Modules:
  0.0 166.1 jit_solution(1090294647130115738)
XLA Ops:
  0.0 1.3 reshape.3.gain
  1.3 94.9 %shard_map.55.hid = bf16[8,64,1792]{2,1,0:T(8,128)(2,1)} custom-call(bf16[64,4096]{1,0:T(8,128)(2,1)} %tok.3, bf16[1,4096]{1,0:T(2,128)(2,1)} %reshape.3.gain, bf16[4096,1792]{1,0:T(8,128)(2,1)} %wg_hbm.1, bf16[4096,1792]{1,0:T(8,128)(2,1)} %wu_hbm.1), custom_call_target="tpu_custom_call" | custom-call | tf_op jit(solution)/shard_map/pallas_call | solution.py:237
  96.3 68.0 %shard_map.56 = bf16[64,4096]{1,0:T(8,128)(2,1)} custom-call(bf16[8,64,1792]{2,1,0:T(8,128)(2,1)} %shard_map.55.hid, bf16[64,4096]{1,0:T(8,128)(2,1)} %tok.3, bf16[1792,4096]{1,0:T(8,128)(2,1)} %wd_hbm.1), custom_call_target="tpu_custom_call" | custom-call | tf_op jit(solution)/shard_map/pallas_call | solution.py:257
  164.2 1.9 %copy.7 = bf16[64,4096]{1,0:T(8,128)(2,1)} copy(bf16[64,4096]{1,0:T(8,128)(2,1)} %shard_map.56) | data formatting | bytes 1048576

commit v2 on v1

--- a/solution.py
+++ b/solution.py
@@ -92,13 +92,7 @@
             up = pb[s, 1, col, :, at].astype(F32) + rv[s, 1, :, at].astype(F32)
             hid[s, :, at] = (gate / (1.0 + jnp.exp(-gate)) * up).astype(BF)
 
-    @pl.loop(0, n)
-    def _(s):
-        @pl.when(s > 0)
-        def _():
-            ring(s - 1, 0).wait_recv()
-            ring(s - 1, 1).wait_recv()
-
+    def pass_on(s):
         @pl.when(s < n - 1)
         def _():
             ring(s, 0).start()
@@ -106,6 +100,11 @@
 
         sib(s, 0).start()
         sib(s, 1).start()
+
+    pass_on(0)
+
+    @pl.loop(0, n)
+    def _(s):
         sib(s, 0).wait_recv()
         sib(s, 1).wait_recv()
 
@@ -118,6 +117,12 @@
         @pl.when(s == 0)
         def _():
             load_u.wait()
+
+        @pl.when(s < n - 1)
+        def _():
+            ring(s, 0).wait_recv()
+            ring(s, 1).wait_recv()
+            pass_on(s + 1)
 
         product(s, 1, wu)
 
@@ -154,13 +159,12 @@
     mine.start()
     rr[n - 1] = jnp.zeros(rr.shape[1:], BF)
     greet((right, left, sibling, across))
-    mine.wait()
 
     def swap(s):
-        return remote(hb.at[col, s], hb.at[col, s], y_s.at[s], y_r.at[s], across)
-
-    def sib(s, d):
-        return remote(pb.at[s, d, 1 - core], r1.at[s, d], sib_s.at[s, d], sib_r.at[s, d], sibling)
+        return remote(hid.at[s], hb.at[col, s], y_s.at[s], y_r.at[s], across)
+
+    def sib(s, d, k):
+        return remote(pb.at[s, d, 1 - core, k], r1.at[s, d, k], sib_s.at[s, d, k], sib_r.at[s, d, k], sibling)
 
     def ring(s, d, k):
         return remote(sn.at[s, d, k], rr.at[s - 1, d, k], ring_s.at[s, d, k], ring_r.at[s, d, k], (left, right)[d])
@@ -169,46 +173,53 @@
     def _(i):
         swap(n - 1 - i).start()
 
+    mine.wait()
     load.wait()
 
-    def product(s):
-        swap(s).wait_recv()
-
-        for k in range(2):
-            @pl.loop(0, piece // tile)
-            def _(t):
-                start = pl.multiple_of(t * tile, tile)
-                w = wd[:, pl.ds(pl.multiple_of(k * piece + t * tile, tile), tile)]
-                h = jnp.concatenate([hb[0, s], hb[1, s]], axis=0)
-                part = jnp.dot(h, w, preferred_element_type=F32).astype(BF)
-                pb[s, :, :, k, :, pl.ds(start, tile)] = part.reshape(2, 2, half, tile)
-        sib(s, 0).start()
-        sib(s, 1).start()
+    def product(s, k):
+        @pl.loop(0, piece // tile)
+        def _(t):
+            start = pl.multiple_of(t * tile, tile)
+            w = wd[:, pl.ds(pl.multiple_of(k * piece + t * tile, tile), tile)]
+            h = jnp.concatenate([hb[0, s], hb[1, s]], axis=0)
+            part = jnp.dot(h, w, preferred_element_type=F32).astype(BF)
+            pb[s, :, :, k, :, pl.ds(start, tile)] = part.reshape(2, 2, half, tile)
+        sib(s, 0, k).start()
+        sib(s, 1, k).start()
 
     def added(s, d, k):
         return pb[s, d, core, k].astype(F32) + r1[s, d, k].astype(F32) + rr[s, d, k].astype(F32)
 
-    product(n - 1)
-
-    @pl.loop(0, n - 1)
+    def stage(s, k):
+        for d in range(2):
+            sib(s, d, k).wait_recv()
+
+            @pl.when(s < n - 1)
+            def _():
+                ring(s + 1, d, k).wait_recv()
+
+            sn[s, d, k] = added(s, d, k).astype(BF)
+            ring(s, d, k).start()
+
+    @pl.loop(0, n)
     def _(i):
         s = n - 1 - i
-        product(s - 1)
-        sib(s, 0).wait_recv()
-        sib(s, 1).wait_recv()
-        for k in range(2):
-            for d in range(2):
-                @pl.when(s < n - 1)
-                def _():
-                    ring(s + 1, d, k).wait_recv()
-
-                sn[s, d, k] = added(s, d, k).astype(BF)
-                ring(s, d, k).start()
-
-    sib(0, 0).wait_recv()
-    sib(0, 1).wait_recv()
+        swap(s).wait_recv()
+        product(s, 0)
+
+        @pl.when(i > 0)
+        def _():
+            stage(s + 1, 1)
+
+        product(s, 1)
+
+        @pl.when(s > 0)
+        def _():
+            stage(s, 0)
+
     for k in range(2):
         for d in range(2):
+            sib(0, d, k).wait_recv()
             ring(1, d, k).wait_recv()
             here = (slice(d * half, (d + 1) * half), slice(k * piece, (k + 1) * piece))
             out[here] = (tok[here].astype(F32) + added(0, d, k)).astype(BF)
@@ -217,7 +228,8 @@
     def _(s):
         swap(s).wait_send()
         for d in range(2):
-            sib(s, d).wait_send()
+            for k in range(2):
+                sib(s, d, k).wait_send()
 
         @pl.when(s > 0)
         def _():
@@ -267,7 +279,7 @@
             pltpu.VMEM((n, 2, 2, half, width // 2), BF),
             pltpu.VMEM((n, 2, 2, half, width // 2), BF),
             dma, dma,
-            dma((n,)), dma((n,)), dma((n, 2)), dma((n, 2)), dma((n, 2, 2)), dma((n, 2, 2)),
+            dma((n,)), dma((n,)), dma((n, 2, 2)), dma((n, 2, 2)), dma((n, 2, 2)), dma((n, 2, 2)),
         ],
         compiler_params=pltpu.CompilerParams(
             collective_id=1, has_side_effects=True, vmem_limit_bytes=60 * 1024 * 1024

time: 166 us -> 157 us (0.946)
  Pallas kernels: 163 us -> 154 us
    pallas_call x1, Pallas kernels: 68 us -> 58.5 us  [kernels(): pl.pallas_call(functools.partial(second_kernel, rows, 256), out_shape=jax...]
where the time goes in v2:
time: 157 us
  Pallas kernels  154 us (98%)
  local copies, waits for them, and re-layouts  3.18 us (2%)
    pallas_call x1, Pallas kernels, kernels(): pl.pallas_call(functools.partial(first_kernel, rows, cols, tile), out_sha...  95.4 us
    pallas_call x1, Pallas kernels, kernels(): pl.pallas_call(functools.partial(second_kernel, rows, 256), out_shape=jax...  58.5 us

profile of v2, /device:TPU:0, one launch (start us, length us, event | category | flops | bytes accessed | tf_op | source)
XLA Modules:
  0.0 157.1 jit_solution(11033407475791327460)
XLA Ops:
  0.0 1.3 reshape.3.gain
  1.3 95.4 %shard_map.55.hid = bf16[8,64,1792]{2,1,0:T(8,128)(2,1)} custom-call(bf16[64,4096]{1,0:T(8,128)(2,1)} %tok.3, bf16[1,4096]{1,0:T(2,128)(2,1)} %reshape.3.gain, bf16[4096,1792]{1,0:T(8,128)(2,1)} %wg_hbm.1, bf16[4096,1792]{1,0:T(8,128)(2,1)} %wu_hbm.1), custom_call_target="tpu_custom_call" | custom-call | tf_op jit(solution)/shard_map/pallas_call | solution.py:249
  96.7 58.5 %shard_map.56 = bf16[64,4096]{1,0:T(8,128)(2,1)} custom-call(bf16[8,64,1792]{2,1,0:T(8,128)(2,1)} %shard_map.55.hid, bf16[64,4096]{1,0:T(8,128)(2,1)} %tok.3, bf16[1792,4096]{1,0:T(8,128)(2,1)} %wd_hbm.1), custom_call_target="tpu_custom_call" | custom-call | tf_op jit(solution)/shard_map/pallas_call | solution.py:269
  155.2 1.9 %copy.7 = bf16[64,4096]{1,0:T(8,128)(2,1)} copy(bf16[64,4096]{1,0:T(8,128)(2,1)} %shard_map.56) | data formatting | bytes 1048576
